TPU v7x, 512 devices: a whole 4x4x16 slice. The times are simulated.
512 devices in a mesh: inst: 16 (over x, z_hi, core), shard: 32 (over y, z_lo).
Axes of the slice: x: 4, y: 4, z: 16 (z_hi: 2, z_lo: 8; z = z_hi * 8 + z_lo), core: 2. Of those that a mesh axis runs over, the one named last changes fastest.
Arguments:
- tokens: bfloat16 [32768, 5120], P(('inst', 'shard')), may hold values from -600 to 600
- norm_gain: float32 [5120], P(('inst', 'shard')), may hold values from 0.1 to 1.9
- master_qkv: float32 [5120, 7168], P(('inst', 'shard')), may hold values from -0.078125 to 0.078125
- qkv_bias: float32 [7168], P(('inst', 'shard')), may hold values from -3 to 3
Outputs:
- qkv_out: bfloat16 [512, 512, 896], P(('inst', 'shard'))
All inputs are finite; a program needn't handle non-finite values.
Results may differ from a plain program's by a relative error of at most 0.0062.
Values may be sent and summed in bfloat16 or wider, within the bound.
No kernel may reach another device: no remote copies, remote signals or barrier semaphores. Data moves between devices by JAX's collectives and lax.ppermute only.
A program may use at most 64 MiB of HBM per device.

v0:
```python
import jax
import jax.numpy as jnp
from jax import lax
from jax.sharding import PartitionSpec as P

QHEADS = 40
KVHEADS = 8
HEAD_DIM = 128
TP = 8


EPSILON = 1e-06


def joined_along(parts, dim):
    dims = list(parts.shape[1:])
    dims[dim] *= parts.shape[0]
    return jnp.moveaxis(parts, 0, dim).reshape(dims)


def gather_packed(arrays, axis, dims):
    ravelled = jnp.concatenate([a.reshape(-1) for a in arrays])
    lines, at, done = (lax.all_gather(ravelled, axis), 0, [])
    for a, dim in zip(arrays, dims):
        parts = lines[:, at : at + a.size].reshape(-1, *a.shape)
        done.append(joined_along(parts, dim))
        at += a.size
    return tuple(done)


def partner_2(value, axis, distance):
    mask = 2**distance
    pairs = [(source, source ^ mask) for source in range(lax.axis_size(axis))]
    return lax.ppermute(value, axis, pairs)


def rank_columns(matrix):
    query_cols = QHEADS * HEAD_DIM
    pair_cols = KVHEADS * HEAD_DIM
    leading = matrix.shape[:-1]
    query = matrix[..., :query_cols].reshape(leading + (TP, query_cols // TP))
    keys = matrix[..., query_cols : query_cols + pair_cols].reshape(leading + (TP, pair_cols // TP))
    values = matrix[..., query_cols + pair_cols :].reshape(leading + (TP, pair_cols // TP))
    return jnp.concatenate([query, keys, values], axis=-1)


def normalize(tokens, gain):
    floats = tokens.astype(jnp.float32)
    scale = lax.rsqrt(jnp.mean(floats * floats, axis=-1, keepdims=True) + EPSILON)
    return (floats * scale * gain.astype(jnp.float32)).astype(jnp.bfloat16)


def per_device(tokens, norm_gain, master_qkv, qkv_bias):
    shard_count = lax.axis_size("shard")
    local_rows = master_qkv.shape[0]
    rank_width = master_qkv.shape[1] // TP
    token_rows = tokens.shape[0]
    gain_full, bias_full = gather_packed(
        (norm_gain.astype(jnp.bfloat16), qkv_bias.astype(jnp.bfloat16)), ("inst", "shard"), (0, 0)
    )
    normed = normalize(tokens, gain_full)
    shard_pos = lax.axis_index("shard")
    rank_index = shard_pos % TP
    bit_count = TP.bit_length() - 1
    bit_order = list(range(bit_count - 1, -1, -1))
    group_rows = normed
    for bit_pos in bit_order:
        partner = partner_2(group_rows, "shard", bit_pos)
        lower = jnp.bitwise_and(jnp.right_shift(shard_pos, bit_pos), 1) == 0
        group_rows = jnp.where(
            lower,
            jnp.concatenate([group_rows, partner], 0),
            jnp.concatenate([partner, group_rows], 0),
        )
    copies = shard_count // TP
    inst_block = shard_count * local_rows
    rows_low = master_qkv.astype(jnp.bfloat16)
    ranked = jnp.transpose(rank_columns(rows_low), (1, 0, 2))
    spread = jnp.broadcast_to(ranked[None], (copies,) + ranked.shape)
    outgoing = spread.reshape(shard_count, rows_low.shape[0], rank_width)
    arrived = lax.all_to_all(outgoing, "shard", split_axis=0, concat_axis=0, tiled=True).reshape(
        inst_block, rank_width
    )
    product = jnp.dot(
        group_rows,
        lax.all_gather(arrived, "inst", axis=0, tiled=True),
        preferred_element_type=jnp.float32,
    )
    bias_ranks = rank_columns(bias_full)
    bias_mine = lax.dynamic_index_in_dim(bias_ranks, rank_index, 0, keepdims=False)
    result = (product + bias_mine.astype(jnp.float32)).astype(jnp.bfloat16)
    shaped = result.reshape((2,) * bit_count + (token_rows, rank_width))
    axes_order = tuple(range(bit_count - 1, -1, -1)) + (bit_count, bit_count + 1)
    result = jnp.transpose(shaped, axes_order).reshape(TP * token_rows, rank_width)
    return result[None]


def solution(mesh):
    in_specs = (
        P(("inst", "shard"), None),
        P(("inst", "shard")),
        P(("inst", "shard"), None),
        P(("inst", "shard")),
    )
    out_specs = P(("inst", "shard"), None, None)
    return jax.shard_map(
        per_device, mesh=mesh, in_specs=in_specs, out_specs=out_specs, check_vma=False
    )
```

profile of v0, /device:TPU:1, one launch (start us, length us, event | category | flops | bytes accessed | tf_op | source)
XLA Modules:
  0.0 480.4 jit_solution(17949804938373927515)
XLA Ops:
  6.5 0.0 all-gather.3.cloned.1.call-start
  6.5 1.0 convert_element_type.36
  7.7 0.0 copy-start.1
  7.8 0.0 copy-start.2
  7.8 0.1 broadcast_in_dim.2
  7.9 0.0 copy-start
  7.9 61.2 %all_to_all.5 = bf16[32,10,896]{2,1,0:T(8,128)(2,1)S(1)} all-to-all(bf16[32,10,896]{2,1,0:T(8,128)(2,1)S(1)} %bitcast.17), channel_id=1, replica_groups=mesh['inst'=16,'shard'=32] {'shard'}, dimensions={0} | all-to-all | bytes 1146880 | tf_op jit(solution)/shard_map/all_to_all | solution.py:81
  69.1 1.0 reshape.51
  70.1 0.0 all-gather.3.cloned.1.call-update
  70.1 0.0 copy-done.1
  70.1 0.0 copy-done.2
  70.2 0.1 pad_maximum_fusion
  70.3 0.2 dynamic-update-slice
  70.5 206.6 %all-reduce = bf16[12288]{0:T(1024)(128)(2,1)S(1)} all-reduce(bf16[12288]{0:T(1024)(128)(2,1)S(1)} %dynamic-update-slice), channel_id=2, replica_groups=mesh['inst'=16,'shard'=32] {'inst','shard'}, use_global_device_ids=true, to_apply=%add | all-reduce | flops 12288 | bytes 49152
  277.1 0.2 reshape.57
  277.3 0.2 reshape.55
  277.5 0.0 copy-done
  277.5 0.2 fusion.7
  277.8 0.2 fusion.9
  278.0 4.8 %collective-permute-start = (bf16[64,5120]{1,0:T(8,128)(2,1)S(1)}, bf16[64,5120]{1,0:T(8,128)(2,1)S(1)}, u32[]{:S(2)}, u32[]{:S(2)}) collective-permute-start(bf16[64,5120]{1,0:T(8,128)(2,1)S(1)} %fusion.9), channel_id=1, source_target_pairs={{0,4},{1,5},{2,6},{3,7},{4,0},{5,1},{6,2},{7,3},{8,12},{9,13},{10,... | collective-permute-start | bytes 1966088 | tf_op jit(solution)/shard_map/ppermute | solution.py:34
  282.9 59.2 %collective-permute-done = bf16[64,5120]{1,0:T(8,128)(2,1)S(1)} collective-permute-done((bf16[64,5120]{1,0:T(8,128)(2,1)S(1)}, bf16[64,5120]{1,0:T(8,128)(2,1)S(1)}, u32[]{:S(2)}, u32[]{:S(2)}) %collective-permute-start) | collective-permute-done | bytes 655392 | tf_op jit(solution)/shard_map/ppermute | solution.py:34
  342.1 0.3 maximum_select_fusion.5
  342.3 1.9 collective-permute-start.1
  344.3 55.5 %collective-permute-done.1 = bf16[128,5120]{1,0:T(8,128)(2,1)S(1)} collective-permute-done((bf16[128,5120]{1,0:T(8,128)(2,1)S(1)}, bf16[128,5120]{1,0:T(8,128)(2,1)S(1)}, u32[]{:S(2)}, u32[]{:S(2)}) %collective-permute-start.1) | collective-permute-done | bytes 1310752 | tf_op jit(solution)/shard_map/ppermute | solution.py:34
  399.8 2.0 maximum_select_fusion.2
  401.7 1.9 collective-permute-start.2
  403.7 0.1 slice.41
  403.8 0.2 slice.34
  404.0 0.2 reshape.52
  404.3 57.5 %collective-permute-done.2 = bf16[256,5120]{1,0:T(8,128)(2,1)S(1)} collective-permute-done((bf16[256,5120]{1,0:T(8,128)(2,1)}, bf16[256,5120]{1,0:T(8,128)(2,1)S(1)}, u32[]{:S(2)}, u32[]{:S(2)}) %collective-permute-start.2) | collective-permute-done | bytes 2621472 | tf_op jit(solution)/shard_map/ppermute | solution.py:34
  461.8 10.8 %add_convert_fusion = bf16[512,896]{1,0:T(8,128)(2,1)S(1)} fusion(bf16[5120,896]{1,0:T(8,128)(2,1)} %all-gather.3.cloned.1.call-done, bf16[256,5120]{1,0:T(8,128)(2,1)S(1)} %collective-permute-done.2, bf16[256,5120]{1,0:T(8,128)(2,1)} %maximum_select_fusion.2, pred[]{:T(512)S(6)} %eq.11, f32[896]{0:T(1024)S(1)} %convert_reduce_fusion), kind=kOutput, calls=%fused_computation.9 | convolution fusion | flops 4722130944 | bytes 15339009 | tf_op jit(solution)/shard_map/dot_general | solution.py:84
  472.5 1.0 copy.8
  (20 shorter events, 0.2 us)
Async XLA Ops:
  6.5 455.2 %all-gather.3.cloned.1.call-start = ((), (), s32[]{:S(2)}) async-start(), calls=%async_computation.1 | async-start | bytes 9748480 | tf_op jit(solution)/shard_map/all_gather | solution.py:86
  7.7 62.4 %copy-start.1 = (f32[10]{0:T(128)S(1)}, f32[10]{0:T(128)}, u32[]{:S(2)}) copy-start(f32[10]{0:T(128)} %param.5) | copy-start | bytes 124
  7.8 62.4 %copy-start.2 = (f32[14]{0:T(128)S(1)}, f32[14]{0:T(128)}, u32[]{:S(2)}) copy-start(f32[14]{0:T(128)} %param.7) | copy-start | bytes 172
  7.9 269.6 %copy-start = (bf16[64,5120]{1,0:T(8,128)(2,1)S(1)}, bf16[64,5120]{1,0:T(8,128)(2,1)}, u32[]{:S(2)}) copy-start(bf16[64,5120]{1,0:T(8,128)(2,1)} %param.4) | copy-start | bytes 1966084
  278.0 64.1 %collective-permute-start = (bf16[64,5120]{1,0:T(8,128)(2,1)S(1)}, bf16[64,5120]{1,0:T(8,128)(2,1)S(1)}, u32[]{:S(2)}, u32[]{:S(2)}) collective-permute-start(bf16[64,5120]{1,0:T(8,128)(2,1)S(1)} %fusion.9), channel_id=1, source_target_pairs={{0,4},{1,5},{2,6},{3,7},{4,0},{5,1},{6,2},{7,3},{8,12},{9,13},{10,... | collective-permute-start | bytes 1966088 | tf_op jit(solution)/shard_map/ppermute | solution.py:34
  342.3 57.5 %collective-permute-start.1 = (bf16[128,5120]{1,0:T(8,128)(2,1)S(1)}, bf16[128,5120]{1,0:T(8,128)(2,1)S(1)}, u32[]{:S(2)}, u32[]{:S(2)}) collective-permute-start(bf16[128,5120]{1,0:T(8,128)(2,1)S(1)} %maximum_select_fusion.5), channel_id=1, source_target_pairs={{0,2},{1,3},{2,0},{3,1},{4,6},{5,7},{6,4},{7,5},{8,10},{9,11},{10,... | collective-permute-start | bytes 3932168 | tf_op jit(solution)/shard_map/ppermute | solution.py:34
  401.7 60.0 %collective-permute-start.2 = (bf16[256,5120]{1,0:T(8,128)(2,1)}, bf16[256,5120]{1,0:T(8,128)(2,1)S(1)}, u32[]{:S(2)}, u32[]{:S(2)}) collective-permute-start(bf16[256,5120]{1,0:T(8,128)(2,1)} %maximum_select_fusion.2), channel_id=1, source_target_pairs={{0,1},{1,0},{2,3},{3,2},{4,5},{5,4},{6,7},{7,6},{8,9},{9,8},{10,11... | collective-permute-start | bytes 7864328 | tf_op jit(solution)/shard_map/ppermute | solution.py:34
Sparse Core Ops, SparseCore 0:
  70.2 188.9 all-gather.2
where the time goes:
time: 481 us; the launch traced here: 480 us
  blocking collectives  268 us (56%)
  waiting for transfers between devices  172 us (36%)
  between operations  13.7 us (3%)
  matrix products  10.8 us (2%)
  starting transfers between devices  8.67 us (2%)
    unnamed x1, blocking collectives  207 us
    ppermute x3, waiting for transfers between devices, partner_2(): return lax.ppermute(value, axis, pairs)  172 us
    all_to_all x1, blocking collectives, per_device(): lax.all_to_all(outgoing, 'shard', split_axis=0, concat_axis=0, tiled=True)  61.2 us
    dot_general x1, matrix products, per_device(): jnp.dot(group_rows, lax.all_gather(arrived, 'inst', axis=0, tiled=True),...  10.8 us
  transfers between devices with their start and end apart: 4, of which 3 were waited for; matrix products, arithmetic and copies ran while one was open for 1% of the time, Pallas kernels for 0%

commit v1 on v0

v1 whole, which is shorter than its diff:
```python
import jax
import jax.numpy as jnp
from jax import lax
from jax.sharding import Mesh
from jax.sharding import PartitionSpec as P

QHEADS = 40
KVHEADS = 8
HEAD_DIM = 128
TP = 8
EPSILON = 1e-06

ZLINE = ("zhi", "zlo")
PLANE = ("x", "core", "y")
ALL = ("x", "zhi", "core", "y", "zlo")


def rank_columns(matrix):
    query_cols = QHEADS * HEAD_DIM
    pair_cols = KVHEADS * HEAD_DIM
    leading = matrix.shape[:-1]
    query = matrix[..., :query_cols].reshape(leading + (TP, query_cols // TP))
    keys = matrix[..., query_cols : query_cols + pair_cols].reshape(leading + (TP, pair_cols // TP))
    values = matrix[..., query_cols + pair_cols :].reshape(leading + (TP, pair_cols // TP))
    return jnp.concatenate([query, keys, values], axis=-1)


def per_device(tokens, norm_gain, master_qkv, qkv_bias):
    local_rows, width = master_qkv.shape
    rank_width = width // TP
    token_rows, depth = tokens.shape
    floats = tokens.astype(jnp.float32)
    scale = lax.rsqrt(jnp.mean(floats * floats, axis=-1, keepdims=True) + EPSILON)
    normed = (floats * scale).astype(jnp.bfloat16)
    group_rows = lax.all_gather(normed, "zlo", axis=0, tiled=True)

    gain = norm_gain.astype(jnp.bfloat16).astype(jnp.float32)[:, None]
    rows = (gain * master_qkv.astype(jnp.bfloat16).astype(jnp.float32)).astype(jnp.bfloat16)
    device = lax.axis_index(ALL)
    bias_row = lax.dynamic_update_slice(
        jnp.zeros((width,), jnp.bfloat16), qkv_bias.astype(jnp.bfloat16), (device * qkv_bias.shape[0],)
    )
    rows = jnp.concatenate([rows, bias_row[None]], axis=0)
    ranked = jnp.transpose(rank_columns(rows), (1, 0, 2))
    outgoing = jnp.concatenate([ranked, ranked], axis=0)
    arrived = lax.all_to_all(outgoing, ZLINE, split_axis=0, concat_axis=0, tiled=True)
    weight_part = arrived[:, :local_rows].reshape(16 * local_rows, rank_width)
    bias_part = jnp.sum(arrived[:, local_rows].astype(jnp.float32), axis=0).astype(jnp.bfloat16)
    bias_part = jnp.pad(bias_part[None], ((0, 7), (0, 0)))
    sent = jnp.concatenate([weight_part, bias_part], axis=0)
    planes = lax.all_gather(sent, PLANE, axis=0, tiled=False)
    bias_mine = jnp.sum(planes[:, 16 * local_rows].astype(jnp.float32), axis=0)
    weights = planes[:, : 16 * local_rows].reshape(4, 8, 2, 8 * local_rows, rank_width)
    weights = jnp.transpose(weights, (0, 2, 1, 3, 4)).reshape(depth, rank_width)
    product = jnp.dot(group_rows, weights, preferred_element_type=jnp.float32)
    return (product + bias_mine).astype(jnp.bfloat16)[None]


def solution(mesh):
    fine = Mesh(mesh.devices.reshape(4, 2, 2, 4, 8), ALL)
    in_specs = (P(ALL, None), P(ALL), P(ALL, None), P(ALL))
    return jax.shard_map(
        per_device, mesh=fine, in_specs=in_specs, out_specs=P(ALL, None, None), check_vma=False
    )
```

time: 481 us -> 263 us (0.55)
  blocking collectives: 268 us -> 36.3 us
  local copies, waits for them, and re-layouts: 3.32 us -> 16.5 us
  starting transfers between devices: 8.67 us -> 0.04 us
  waiting for transfers between devices: 172 us -> 179 us
    unnamed x1 -> x0, blocking collectives: 207 us -> none
    all_gather x1 -> x2, waiting for transfers between devices: 0.01 us -> 179 us  [the longest x1 108 us: per_device(): group_rows = lax.all_gather(normed, 'zlo', axis=0, tiled=True)]
    ppermute x3 -> x0, waiting for transfers between devices: 172 us -> none  [partner_2(): return lax.ppermute(value, axis, pairs)]
    all_to_all x1, blocking collectives: 61.2 us -> 36.3 us  [per_device(): lax.all_to_all(outgoing, ZLINE, split_axis=0, concat_axis=0, tiled=True)]
    ppermute x3 -> x0, starting transfers between devices: 8.66 us -> none  [partner_2(): return lax.ppermute(value, axis, pairs)]
    slice x6 -> x1, local copies, waits for them, and re-layouts: 0.33 us -> 7.98 us  [per_device(): planes[:, :16 * local_rows].reshape(4, 8, 2, 8 * local_rows, rank_width)]
    transpose x2 -> x1, local copies, waits for them, and re-layouts: 1.03 us -> 8 us  [per_device(): weights = jnp.transpose(weights, (0, 2, 1, 3, 4)).reshape(depth, rank_width)]
  transfers between devices with their start and end apart: 4 -> 2, of which waited for: 3 -> 2; matrix products, arithmetic and copies ran while one was open for 1% -> 7% of each run, Pallas kernels for 0% -> 0%
where the time goes in v1:
time: 263 us
  waiting for transfers between devices  179 us (68%)
  blocking collectives  36.3 us (14%)
  local copies, waits for them, and re-layouts  16.5 us (6%)
  between operations  13.5 us (5%)
  matrix products  11.1 us (4%)
  other arithmetic  5.88 us (2%)
    all_gather x1, waiting for transfers between devices, per_device(): group_rows = lax.all_gather(normed, 'zlo', axis=0, tiled=True)  108 us
    all_gather x1, waiting for transfers between devices, per_device(): planes = lax.all_gather(sent, PLANE, axis=0, tiled=False)  71.5 us
    all_to_all x1, blocking collectives, per_device(): lax.all_to_all(outgoing, ZLINE, split_axis=0, concat_axis=0, tiled=True)  36.3 us
    dot_general x1, matrix products, per_device(): product = jnp.dot(group_rows, weights, preferred_element_type=jnp.float32)  11.1 us
    transpose x1, local copies, waits for them, and re-layouts, per_device(): weights = jnp.transpose(weights, (0, 2, 1, 3, 4)).reshape(depth, rank_width)  8 us
    slice x1, local copies, waits for them, and re-layouts, per_device(): planes[:, :16 * local_rows].reshape(4, 8, 2, 8 * local_rows, rank_width)  7.98 us
  transfers between devices with their start and end apart: 2, of which 2 were waited for; matrix products, arithmetic and copies ran while one was open for 7% of the time, Pallas kernels for 0%

profile of v1, /device:TPU:1, one launch (start us, length us, event | category | flops | bytes accessed | tf_op | source)
XLA Modules:
  0.0 262.7 jit_solution(10151386681148762155)
XLA Ops:
  6.5 0.0 copy-start
  6.5 0.0 all-gather.6.cloned.1.call-start
  6.5 0.7 convert_convert_fusion
  7.3 0.7 convert_bitcast_fusion
  7.9 1.1 multiply_convert_fusion
  9.1 0.3 dynamic_update_slice.4
  9.7 36.3 %all_to_all.5 = bf16[16,11,896]{2,1,0:T(8,128)(2,1)S(1)} all-to-all(bf16[16,11,896]{2,1,0:T(8,128)(2,1)S(1)} %pad_maximum_fusion), channel_id=1, replica_groups=mesh['x'=4,'zhi'=2,'core'=2,'y'=4,'zlo'=8] {'zhi','zlo'}, dimensions={0} | all-to-all | bytes 630784 | tf_op jit(solution)/shard_map/all_to_all | solution.py:46
  46.0 0.1 slice_reduce_fusion
  46.1 0.1 reshape.34
  46.2 0.7 fusion.4
  47.0 0.0 all-gather.6.cloned.1.call-update
  47.0 0.0 all-gather.4.cloned.1.call-start
  47.0 0.0 copy-done
  47.0 0.2 fusion.1
  47.3 1.0 fusion.2
  48.3 0.0 all-gather.4.cloned.1.call-update
  48.3 71.5 %all-gather.6.cloned.1.call-done = bf16[5376,896]{1,0:T(8,128)(2,1)} async-done(((bf16[168,896]{1,0:T(8,128)(2,1)}), bf16[5376,896]{1,0:T(8,128)(2,1)}) %all-gather.6.cloned.1.call-update) | async-done | bytes 9633808 | tf_op jit(solution)/shard_map/all_gather | solution.py:51
  119.8 8.0 %slice.34 = bf16[32,160,896]{2,1,0:T(8,128)(2,1)} slice(bf16[32,168,896]{2,1,0:T(8,128)(2,1)} %bitcast.25), slice={[0:32], [0:160], [0:896]} | slice | bytes 18350080 | tf_op jit(solution)/shard_map/slice | solution.py:53
  127.8 8.0 %copy.11 = bf16[4,2,8,80,896]{4,3,2,1,0:T(8,128)(2,1)} copy(bf16[4,2,8,80,896]{4,3,1,2,0:T(8,128)(2,1)} %bitcast.23) | data formatting | bytes 18350080 | tf_op jit(solution)/shard_map/transpose | solution.py:54
  135.8 1.1 fusion.6
  136.9 107.8 %all-gather.4.cloned.1.call-done = bf16[512,5120]{1,0:T(8,128)(2,1)} async-done(((bf16[64,5120]{1,0:T(8,128)(2,1)}), bf16[512,5120]{1,0:T(8,128)(2,1)}) %all-gather.4.cloned.1.call-update) | async-done | bytes 5242896 | tf_op jit(solution)/shard_map/all_gather | solution.py:35
  244.8 11.1 %fusion = bf16[1,512,896]{2,1,0:T(8,128)(2,1)} fusion(bf16[512,5120]{1,0:T(8,128)(2,1)} %all-gather.4.cloned.1.call-done, bf16[5120,896]{1,0:T(8,128)(2,1)} %bitcast.24, f32[896]{0:T(1024)S(1)} %fusion.6), kind=kOutput, calls=%fused_computation.3 | convolution fusion | flops 4698537984 | bytes 15339008 | tf_op jit(solution)/shard_map/dot_general | solution.py:55
  (16 shorter events, 0.3 us)
Async XLA Ops:
  6.5 40.5 %copy-start = (bf16[64,5120]{1,0:T(8,128)(2,1)S(1)}, bf16[64,5120]{1,0:T(8,128)(2,1)}, u32[]{:S(2)}) copy-start(bf16[64,5120]{1,0:T(8,128)(2,1)} %param.4) | copy-start | bytes 1966084
  6.5 113.3 %all-gather.6.cloned.1.call-start = ((), (), s32[]{:S(2)}) async-start(), calls=%async_computation.2 | async-start | bytes 9934848 | tf_op jit(solution)/shard_map/all_gather | solution.py:51
  47.0 197.8 %all-gather.4.cloned.1.call-start = ((), (), s32[]{:S(2)}) async-start(), calls=%async_computation.1 | async-start | bytes 5898240 | tf_op jit(solution)/shard_map/all_gather | solution.py:35
Sparse Core Ops, SparseCore 0:
  47.1 72.6 all-gather.5
  121.9 122.7 all-gather.3

commit v2 on v1

v2 whole, which is shorter than its diff:
```python
import functools

import jax
import jax.numpy as jnp
from jax import lax
from jax.experimental import pallas as pl
from jax.experimental.pallas import tpu as pltpu
from jax.sharding import Mesh
from jax.sharding import PartitionSpec as P


QHEADS = 40
KVHEADS = 8
TP = 8
EPSILON = 1e-06

ZLINE = ("zhi", "zlo")
PLANE = ("x", "core", "y")
ALL = ("x", "zhi", "core", "y", "zlo")
NX, NZHI, NCORE, NY, NZLO = 4, 2, 2, 4, 8
NZ = NZHI * NZLO
LANES = 128
EARLY = 4
MIB = 1 << 20


def rank_tiles():
    q = QHEADS // TP
    return [
        [r * q + c for c in range(q)] + [QHEADS + r, QHEADS + KVHEADS + r] for r in range(TP)
    ]


def pack_kernel(master_ref, gain_ref, bias_ref, out_ref, line):
    rows = master_ref.shape[0]
    gain = gain_ref[...].astype(jnp.bfloat16).astype(jnp.float32)
    for r, tiles in enumerate(rank_tiles()):
        line[...] = jnp.zeros_like(line)
        for c, t in enumerate(tiles):
            piece = master_ref[:, t * LANES : (t + 1) * LANES]
            line[c * rows : (c + 1) * rows, :] = gain * piece.astype(jnp.bfloat16).astype(jnp.float32)
            at = len(tiles) * rows + c
            line[at : at + 1, :] = bias_ref[t : t + 1, :]
        block = line[...].astype(jnp.bfloat16)
        for h in range(NZHI):
            out_ref[h * TP + r] = block


def pack(master, gain, bias_row):
    rows = master.shape[0]
    return pl.pallas_call(
        pack_kernel,
        out_shape=jax.ShapeDtypeStruct((NZ, 80, LANES), jnp.bfloat16),
        scratch_shapes=[pltpu.VMEM((80, LANES), jnp.float32)],
        compiler_params=pltpu.CompilerParams(vmem_limit_bytes=8 * MIB),
        name="pack",
    )(master, gain.reshape(rows, 1), bias_row)


def unpack_kernel(rows, lines_ref, out_ref, line, wide):
    tiles = wide.shape[1] // LANES
    total = jnp.zeros((8, LANES), jnp.float32)
    for s in range(NZ):
        line[...] = lines_ref[s].astype(jnp.float32)
        for c in range(tiles):
            wide[s * rows : (s + 1) * rows, c * LANES : (c + 1) * LANES] = line[c * rows : (c + 1) * rows, :]
        total = total + line[tiles * rows : tiles * rows + 8, :]
    line[0:8, :] = total
    wide[NZ * rows :, :] = jnp.zeros((8, wide.shape[1]), jnp.float32)
    for c in range(tiles):
        wide[NZ * rows : NZ * rows + 1, c * LANES : (c + 1) * LANES] = line[c : c + 1, :]
    out_ref[...] = wide[...].astype(jnp.bfloat16)


def unpack(lines, rows, width):
    high = NZ * rows + 8
    return pl.pallas_call(
        functools.partial(unpack_kernel, rows),
        out_shape=jax.ShapeDtypeStruct((high, width), jnp.bfloat16),
        scratch_shapes=[pltpu.VMEM((80, LANES), jnp.float32), pltpu.VMEM((high, width), jnp.float32)],
        compiler_params=pltpu.CompilerParams(vmem_limit_bytes=8 * MIB),
        name="unpack",
    )(lines)


def start_weights(planes, wbuf, bbuf, wsem, bsem, run):
    depth = wbuf.shape[0]
    chunk = depth // NX
    for x in range(NX):
        for h in range(NZHI):
            for c in range(NCORE):
                for y in range(NY):
                    at = (((x * NZHI + h) * NCORE + c) * NY + y) * run
                    pltpu.make_async_copy(
                        planes.at[(x * NCORE + c) * NY + y, h * run : (h + 1) * run],
                        wbuf.at[at : at + run],
                        wsem.at[x],
                    ).start()
    bias_copy = pltpu.make_async_copy(planes.at[:, NZHI * run : NZHI * run + 8], bbuf, bsem)
    bias_copy.start()
    return chunk, bias_copy


def multiply(x, wbuf, bbuf, acc, wsem, bias_copy, chunk):
    def step(i, _):
        here = pl.ds(pl.multiple_of(i * chunk, chunk), chunk)
        pltpu.make_async_copy(wbuf.at[here], wbuf.at[here], wsem.at[i]).wait()
        part = jnp.dot(x[:, here], wbuf[here, :], preferred_element_type=jnp.float32)

        @pl.when(i == 0)
        def _():
            acc[...] = part

        @pl.when(i > 0)
        def _():
            acc[...] += part

        return 0

    lax.fori_loop(0, NX, step, 0)
    bias_copy.wait()
    bias = jnp.sum(jnp.sum(bbuf[...].astype(jnp.float32), axis=0), axis=0, keepdims=True)
    return (acc[...] + bias).astype(jnp.bfloat16)


def token_copies(slots, x, sems, half):
    copies = []
    for i, (refs, cond, row) in enumerate(slots):
        for h, ref in enumerate(refs):
            at = pl.multiple_of(row + h * half, 8)
            copies.append((cond, pltpu.make_async_copy(ref, x.at[pl.ds(at, half)], sems.at[2 * i + h])))
    return copies


def start_all(copies):
    for cond, copy in copies:
        pl.when(cond)(copy.start)


def wait_all(copies):
    for cond, copy in copies:
        pl.when(cond)(copy.wait)


def early_kernel(half, run, *refs):
    planes = refs[0]
    own = refs[1:3]
    left = [refs[3 + 2 * s : 5 + 2 * s] for s in range(EARLY)]
    right = [refs[3 + 2 * EARLY + 2 * s : 5 + 2 * EARLY + 2 * s] for s in range(EARLY)]
    out_ref, x, wbuf, bbuf, acc, wsem, bsem, xsem = refs[3 + 4 * EARLY :]
    me = lax.axis_index("zlo")
    chunk, bias_copy = start_weights(planes, wbuf, bbuf, wsem, bsem, run)
    block = 2 * half
    slots = [(own, me >= 0, me * block)]
    for s in range(1, EARLY + 1):
        slots.append((left[s - 1], me >= s, jnp.maximum(me - s, 0) * block))
        slots.append((right[s - 1], me + s < NZLO, jnp.minimum(me + s, NZLO - 1) * block))
    copies = token_copies(slots, x, xsem, half)
    start_all(copies)
    wait_all(copies)
    out_ref[...] = multiply(x, wbuf, bbuf, acc, wsem, bias_copy, chunk)


def late_kernel(half, run, *refs):
    late = NZLO - 1 - EARLY
    planes = refs[0]
    left = [refs[1 + 2 * s : 3 + 2 * s] for s in range(late)]
    right = [refs[1 + 2 * late + 2 * s : 3 + 2 * late + 2 * s] for s in range(late)]
    _, out_ref, x, wbuf, bbuf, acc, obuf, wsem, bsem, xsem, osem = refs[1 + 4 * late :]
    me = lax.axis_index("zlo")
    chunk, bias_copy = start_weights(planes, wbuf, bbuf, wsem, bsem, run)
    block = 2 * half
    copies = []
    for s in range(late):
        dist = EARLY + 1 + s
        copies += token_copies(
            [(left[s], me >= dist, s * block), (right[s], me + dist < NZLO, s * block)],
            x, xsem.at[s], half,
        )
    start_all(copies)
    wait_all(copies)
    obuf[...] = multiply(x, wbuf, bbuf, acc, wsem, bias_copy, chunk)
    outs = []
    for s in range(late):
        dist = EARLY + 1 + s
        go_left, go_right = me >= dist, me + dist < NZLO
        place = jnp.clip(jnp.where(go_left, me - dist, me + dist), 0, NZLO - 1)
        copy = pltpu.make_async_copy(
            obuf.at[s * block : (s + 1) * block],
            out_ref.at[pl.ds(pl.multiple_of(place * block, block), block)],
            osem.at[s],
        )
        outs.append((jnp.logical_or(go_left, go_right), copy))
    start_all(outs)
    wait_all(outs)


def common_scratch(rows, depth, width):
    return [
        pltpu.VMEM((rows, depth), jnp.bfloat16),
        pltpu.VMEM((depth, width), jnp.bfloat16),
        pltpu.VMEM((NX * NCORE * NY, 8, width), jnp.bfloat16),
        pltpu.VMEM((rows, width), jnp.float32),
    ]


def early_call(planes, own, left, right, run):
    half, depth = own[0].shape
    width = planes.shape[-1]
    rows = 2 * half * NZLO
    flat = [a for pair in [own] + left + right for a in pair]
    return pl.pallas_call(
        functools.partial(early_kernel, half, run),
        out_shape=jax.ShapeDtypeStruct((rows, width), jnp.bfloat16),
        in_specs=[pl.BlockSpec(memory_space=pltpu.HBM)] * (1 + len(flat)),
        scratch_shapes=common_scratch(rows, depth, width) + [
            pltpu.SemaphoreType.DMA((NX,)),
            pltpu.SemaphoreType.DMA,
            pltpu.SemaphoreType.DMA((2 * (1 + 2 * EARLY),)),
        ],
        compiler_params=pltpu.CompilerParams(vmem_limit_bytes=26 * MIB),
        cost_estimate=pl.CostEstimate(flops=2 * rows * depth * width, bytes_accessed=2 * depth * width, transcendentals=0),
        name="early",
    )(planes, *flat)


def late_call(planes, left, right, before, run):
    half, depth = left[0][0].shape
    width = planes.shape[-1]
    late = len(left)
    rows = 2 * half * late
    flat = [a for pair in left + right for a in pair]
    return pl.pallas_call(
        functools.partial(late_kernel, half, run),
        out_shape=jax.ShapeDtypeStruct(before.shape, jnp.bfloat16),
        in_specs=[pl.BlockSpec(memory_space=pltpu.HBM)] + [pl.BlockSpec(memory_space=pl.ANY)] * (1 + len(flat)),
        out_specs=pl.BlockSpec(memory_space=pl.ANY),
        input_output_aliases={1 + len(flat): 0},
        scratch_shapes=common_scratch(rows, depth, width) + [
            pltpu.VMEM((rows, width), jnp.bfloat16),
            pltpu.SemaphoreType.DMA((NX,)),
            pltpu.SemaphoreType.DMA,
            pltpu.SemaphoreType.DMA((late, 4)),
            pltpu.SemaphoreType.DMA((late,)),
        ],
        compiler_params=pltpu.CompilerParams(vmem_limit_bytes=20 * MIB),
        cost_estimate=pl.CostEstimate(flops=2 * rows * depth * width, bytes_accessed=2 * depth * width, transcendentals=0),
        name="late",
    )(planes, *flat, before)


def project(tokens, norm_gain, master_qkv, qkv_bias):
    local_rows, width = master_qkv.shape
    rank_width = width // TP
    token_rows, _ = tokens.shape
    half = token_rows // 2
    floats = tokens.astype(jnp.float32)
    scale = lax.rsqrt(jnp.mean(floats * floats, axis=-1, keepdims=True) + EPSILON)
    normed = (floats * scale).astype(jnp.bfloat16)
    own = [normed[:half], normed[half:]]

    to_right, to_left = [own], [own]
    for s in range(1, NZLO):
      up = [(k, k + 1) for k in range(s - 1, NZLO - 1)]
      down = [(k, k - 1) for k in range(1, NZLO - s + 1)]
      moved_right, moved_left = [], []
      for h in range(2):
          moved_right.append(lax.ppermute(to_right[-1][h], "zlo", up))
          moved_left.append(lax.ppermute(to_left[-1][h], "zlo", down))
      to_right.append(moved_right)
      to_left.append(moved_left)
    from_left, from_right = to_right[1:], to_left[1:]

    device = lax.axis_index(ALL)
    bias_row = lax.dynamic_update_slice(
        jnp.zeros((width,), jnp.float32),
        qkv_bias.astype(jnp.bfloat16).astype(jnp.float32),
        (device * qkv_bias.shape[0],),
    ).reshape(width // LANES, LANES)
    master_qkv, own[0], own[1] = lax.optimization_barrier((master_qkv, own[0], own[1]))
    lines = pack(master_qkv, norm_gain, bias_row)
    arrived = lax.all_to_all(lines, ZLINE, split_axis=0, concat_axis=0, tiled=True)
    block = unpack(arrived, local_rows, rank_width)
    planes = lax.all_gather(block, PLANE, axis=0, tiled=False)

    run = NZLO * local_rows
    first = early_call(planes, own, from_left[:EARLY], from_right[:EARLY], run)
    result = late_call(planes, from_left[EARLY:], from_right[EARLY:], first, run)
    return result[None]


def solution(mesh):
    fine = Mesh(mesh.devices.reshape(NX, NZHI, NCORE, NY, NZLO), ALL)
    in_specs = (P(ALL, None), P(ALL), P(ALL, None), P(ALL))
    return jax.shard_map(project, mesh=fine, in_specs=in_specs, out_specs=P(ALL, None, None), check_vma=False)
```

time: 263 us -> 215 us (0.82)
  the two profiles are of different devices: /device:TPU:1 before, /device:TPU:34 now
where the time goes in v2:
time: 215 us; the launch traced here: 214 us
  starting transfers between devices  60.1 us (28%)
  Pallas kernels  41.2 us (19%)
  blocking collectives  34.9 us (16%)
  local copies, waits for them, and re-layouts  31 us (14%)
  waiting for transfers between devices  29.6 us (14%)
  between operations  13.9 us (6%)
  other arithmetic  2.76 us (1%)
    ppermute x14, starting transfers between devices, project(): moved_left.append(lax.ppermute(to_left[-1][h], 'zlo', down))  36.7 us
    all_to_all x1, blocking collectives, project(): lax.all_to_all(lines, ZLINE, split_axis=0, concat_axis=0, tiled=True)  34.9 us
    unnamed x74, local copies, waits for them, and re-layouts  30.9 us
    ppermute x14, waiting for transfers between devices, project(): moved_left.append(lax.ppermute(to_left[-1][h], 'zlo', down))  27.3 us
    pallas_call x1, Pallas kernels, early_call(): pl.pallas_call(functools.partial(early_kernel, half, run), out_shape=jax....  23.9 us
    ppermute x14, starting transfers between devices, project(): moved_right.append(lax.ppermute(to_right[-1][h], 'zlo', up))  23.4 us
    pallas_call x1, Pallas kernels, late_call(): pl.pallas_call(functools.partial(late_kernel, half, run), out_shape=jax.S...  16.3 us
  transfers between devices with their start and end apart: 29, of which 11 were waited for; matrix products, arithmetic and copies ran while one was open for 0% of the time, Pallas kernels for 11%

profile of v2, /device:TPU:34, one launch (start us, length us, event | category | flops | bytes accessed | tf_op | source)
XLA Modules:
  0.0 213.5 jit_solution(9654919366413095984)
XLA Ops:
  9.7 34.9 %all_to_all.5.lines_ref = bf16[16,80,128]{2,1,0:T(8,128)(2,1)S(1)} all-to-all(bf16[16,80,128]{2,1,0:T(8,128)(2,1)S(1)} %pack.1), channel_id=1, replica_groups=mesh['x'=4,'zhi'=2,'core'=2,'y'=4,'zlo'=8] {'zhi','zlo'}, dimensions={0} | all-to-all | bytes 655360 | tf_op jit(solution)/shard_map/all_to_all | solution.py:282
  45.5 4.1 %collective-permute-start = (bf16[32,5120]{1,0:T(8,128)(2,1)S(1)}, bf16[32,5120]{1,0:T(8,128)(2,1)S(1)}, u32[]{:S(2)}, u32[]{:S(2)}) collective-permute-start(bf16[32,5120]{1,0:T(8,128)(2,1)S(1)} %get-tuple-element.9.refs_1_), channel_id=1, source_target_pairs={{0,1},{1,2},{2,3},{3,4},{4,5},{5,6},{6,7},{8,9},{9,10},{10,11},{11... | collective-permute-start | bytes 983048 | tf_op jit(solution)/shard_map/ppermute | solution.py:268
  49.6 2.8 %collective-permute-start.5 = (bf16[32,5120]{1,0:T(8,128)(2,1)S(1)}, bf16[32,5120]{1,0:T(8,128)(2,1)S(1)}, u32[]{:S(2)}, u32[]{:S(2)}) collective-permute-start(bf16[32,5120]{1,0:T(8,128)(2,1)S(1)} %get-tuple-element.10.refs_2_), channel_id=1, source_target_pairs={{0,1},{1,2},{2,3},{3,4},{4,5},{5,6},{6,7},{8,9},{9,10},{10,11},{11... | collective-permute-start | bytes 983048 | tf_op jit(solution)/shard_map/ppermute | solution.py:268
  52.4 3.0 %collective-permute-start.14 = (bf16[32,5120]{1,0:T(8,128)(2,1)S(1)}, bf16[32,5120]{1,0:T(8,128)(2,1)S(1)}, u32[]{:S(2)}, u32[]{:S(2)}) collective-permute-start(bf16[32,5120]{1,0:T(8,128)(2,1)S(1)} %get-tuple-element.9.refs_1_), channel_id=1, source_target_pairs={{1,0},{2,1},{3,2},{4,3},{5,4},{6,5},{7,6},{9,8},{10,9},{11,10},{12... | collective-permute-start | bytes 983048 | tf_op jit(solution)/shard_map/ppermute | solution.py:269
  55.4 1.9 collective-permute-start.19
  58.0 3.9 %collective-permute-start.1 = (bf16[32,5120]{1,0:T(8,128)(2,1)S(1)}, bf16[32,5120]{1,0:T(8,128)(2,1)S(1)}, u32[]{:S(2)}, u32[]{:S(2)}) collective-permute-start(bf16[32,5120]{1,0:T(8,128)(2,1)S(1)} %collective-permute-done.refs_3_), channel_id=1, source_target_pairs={{1,2},{2,3},{3,4},{4,5},{5,6},{6,7},{9,10},{10,11},{11,12},{12,13}... | collective-permute-start | bytes 983048 | tf_op jit(solution)/shard_map/ppermute | solution.py:268
  62.6 1.7 collective-permute-done.5.refs_4_
  64.3 4.4 %collective-permute-start.6 = (bf16[32,5120]{1,0:T(8,128)(2,1)S(1)}, bf16[32,5120]{1,0:T(8,128)(2,1)S(1)}, u32[]{:S(2)}, u32[]{:S(2)}) collective-permute-start(bf16[32,5120]{1,0:T(8,128)(2,1)S(1)} %collective-permute-done.5.refs_4_), channel_id=1, source_target_pairs={{1,2},{2,3},{3,4},{4,5},{5,6},{6,7},{9,10},{10,11},{11,12},{12,13}... | collective-permute-start | bytes 983048 | tf_op jit(solution)/shard_map/ppermute | solution.py:268
  69.5 1.9 collective-permute-start.15
  72.1 1.9 collective-permute-start.20
  77.6 1.9 collective-permute-done.15.refs_13_
  79.4 3.6 %collective-permute-start.16 = (bf16[32,5120]{1,0:T(8,128)(2,1)S(1)}, bf16[32,5120]{1,0:T(8,128)(2,1)S(1)}, u32[]{:S(2)}, u32[]{:S(2)}) collective-permute-start(bf16[32,5120]{1,0:T(8,128)(2,1)S(1)} %collective-permute-done.15.refs_13_), channel_id=1, source_target_pairs={{1,0},{2,1},{3,2},{4,3},{5,4},{9,8},{10,9},{11,10},{12,11},{13,12}... | collective-permute-start | bytes 983048 | tf_op jit(solution)/shard_map/ppermute | solution.py:269
  83.8 1.9 collective-permute-done.20.refs_14_
  85.7 4.4 %collective-permute-start.21 = (bf16[32,5120]{1,0:T(8,128)(2,1)S(1)}, bf16[32,5120]{1,0:T(8,128)(2,1)S(1)}, u32[]{:S(2)}, u32[]{:S(2)}) collective-permute-start(bf16[32,5120]{1,0:T(8,128)(2,1)S(1)} %collective-permute-done.20.refs_14_), channel_id=1, source_target_pairs={{1,0},{2,1},{3,2},{4,3},{5,4},{9,8},{10,9},{11,10},{12,11},{13,12}... | collective-permute-start | bytes 983048 | tf_op jit(solution)/shard_map/ppermute | solution.py:269
  93.7 3.2 %collective-permute-done.16.refs_15_ = bf16[32,5120]{1,0:T(8,128)(2,1)S(1)} collective-permute-done((bf16[32,5120]{1,0:T(8,128)(2,1)S(1)}, bf16[32,5120]{1,0:T(8,128)(2,1)S(1)}, u32[]{:S(2)}, u32[]{:S(2)}) %collective-permute-start.16) | collective-permute-done | bytes 327712 | tf_op jit(solution)/shard_map/ppermute | solution.py:269
  96.9 1.9 collective-permute-start.17
  99.6 4.4 %collective-permute-done.21.refs_16_ = bf16[32,5120]{1,0:T(8,128)(2,1)S(1)} collective-permute-done((bf16[32,5120]{1,0:T(8,128)(2,1)S(1)}, bf16[32,5120]{1,0:T(8,128)(2,1)S(1)}, u32[]{:S(2)}, u32[]{:S(2)}) %collective-permute-start.21) | collective-permute-done | bytes 327712 | tf_op jit(solution)/shard_map/ppermute | solution.py:269
  103.9 1.9 collective-permute-start.22
  109.4 1.5 collective-permute-done.17.refs_17_
  110.9 1.9 collective-permute-start.18
  113.5 4.4 %collective-permute-done.22.refs_18_ = bf16[32,5120]{1,0:T(8,128)(2,1)S(1)} collective-permute-done((bf16[32,5120]{1,0:T(8,128)(2,1)S(1)}, bf16[32,5120]{1,0:T(8,128)(2,1)S(1)}, u32[]{:S(2)}, u32[]{:S(2)}) %collective-permute-start.22) | collective-permute-done | bytes 327712 | tf_op jit(solution)/shard_map/ppermute | solution.py:269
  117.9 1.9 collective-permute-start.23
  122.0 3.0 %collective-permute-done.18.refs_7_ = bf16[32,5120]{1,0:T(8,128)(2,1)S(1)} collective-permute-done((bf16[32,5120]{1,0:T(8,128)(2,1)S(1)}, bf16[32,5120]{1,0:T(8,128)(2,1)S(1)}, u32[]{:S(2)}, u32[]{:S(2)}) %collective-permute-start.18) | collective-permute-done | bytes 327712 | tf_op jit(solution)/shard_map/ppermute | solution.py:269
  124.9 1.9 collective-permute-start.24
  126.9 5.1 %collective-permute-done.23.refs_8_ = bf16[32,5120]{1,0:T(8,128)(2,1)S(1)} collective-permute-done((bf16[32,5120]{1,0:T(8,128)(2,1)S(1)}, bf16[32,5120]{1,0:T(8,128)(2,1)S(1)}, u32[]{:S(2)}, u32[]{:S(2)}) %collective-permute-start.23) | collective-permute-done | bytes 327712 | tf_op jit(solution)/shard_map/ppermute | solution.py:269
  132.0 1.9 collective-permute-start.25
  136.7 3.4 %collective-permute-start.26 = (bf16[32,5120]{1,0:T(8,128)(2,1)S(1)}, bf16[32,5120]{1,0:T(8,128)(2,1)}, u32[]{:S(2)}, u32[]{:S(2)}) collective-permute-start(bf16[32,5120]{1,0:T(8,128)(2,1)S(1)} %collective-permute-done.24.refs_9_), channel_id=1, source_target_pairs={{1,0},{9,8},{17,16},{25,24},{33,32},{41,40},{49,48},{57,56},{65,64... | collective-permute-start | bytes 983048 | tf_op jit(solution)/shard_map/ppermute | solution.py:269
  140.1 1.9 collective-permute-done.25.refs_10_
  142.0 5.1 %collective-permute-start.27 = (bf16[32,5120]{1,0:T(8,128)(2,1)S(1)}, bf16[32,5120]{1,0:T(8,128)(2,1)}, u32[]{:S(2)}, u32[]{:S(2)}) collective-permute-start(bf16[32,5120]{1,0:T(8,128)(2,1)S(1)} %collective-permute-done.25.refs_10_), channel_id=1, source_target_pairs={{1,0},{9,8},{17,16},{25,24},{33,32},{41,40},{49,48},{57,56},{65,64... | collective-permute-start | bytes 983048 | tf_op jit(solution)/shard_map/ppermute | solution.py:269
  147.1 3.7 %copy-done = bf16[5376,896]{1,0:T(8,128)(2,1)S(1)} copy-done((bf16[5376,896]{1,0:T(8,128)(2,1)S(1)}, bf16[5376,896]{1,0:T(8,128)(2,1)}, u32[]{:S(2)}) %copy-start) | copy-done | bytes 9633816
  166.4 23.9 %early.1.refs_13_ = bf16[512,896]{1,0:T(8,128)(2,1)} custom-call(bf16[32,168,896]{2,1,0:T(8,128)(2,1)S(1)} %bitcast.4, bf16[32,5120]{1,0:T(8,128)(2,1)S(1)} %get-tuple-element.9.refs_1_, bf16[32,5120]{1,0:T(8,128)(2,1)S(1)} %get-tuple-element.10.refs_2_, bf16[32,5120]{1,0:T(8,128)(2,1)S(1)} %copy-done.4, bf16[32,5120]{1,0:T(8,128)(2,1)S(1)} %copy-done.6, ...), custom_call_target="tpu_custom_call" | custom-call | flops 4697620480 | bytes 9175040 | tf_op jit(solution)/shard_map/early/pallas_call | solution.py:212
  190.3 16.3 %late.1 = bf16[512,896]{1,0:T(8,128)(2,1)} custom-call(bf16[32,168,896]{2,1,0:T(8,128)(2,1)S(1)} %bitcast.5, bf16[32,5120]{1,0:T(8,128)(2,1)S(1)} %collective-permute-done.4.refs_1_, bf16[32,5120]{1,0:T(8,128)(2,1)S(1)} %collective-permute-done.9.refs_2_, bf16[32,5120]{1,0:T(8,128)(2,1)S(1)} %collective-permute-done.10.refs_3_, ...), custom_call_target="tpu_custom_call", output_to_operand_aliasing={{}: (13, {})} | custom-call | flops 1761607680 | bytes 9175040 | tf_op jit(solution)/shard_map/late/pallas_call | solution.py:233
  (113 shorter events, 39.9 us)
Async XLA Ops:
  6.5 140.6 %all-gather.3.cloned.1.call-start = ((), (), s32[]{:S(2)}) async-start(), calls=%async_computation.1 | async-start | bytes 9934848 | tf_op jit(solution)/shard_map/all_gather | solution.py:284
  7.9 1.6 copy-start.2
  45.5 12.5 %collective-permute-start = (bf16[32,5120]{1,0:T(8,128)(2,1)S(1)}, bf16[32,5120]{1,0:T(8,128)(2,1)S(1)}, u32[]{:S(2)}, u32[]{:S(2)}) collective-permute-start(bf16[32,5120]{1,0:T(8,128)(2,1)S(1)} %get-tuple-element.9.refs_1_), channel_id=1, source_target_pairs={{0,1},{1,2},{2,3},{3,4},{4,5},{5,6},{6,7},{8,9},{9,10},{10,11},{11... | collective-permute-start | bytes 983048 | tf_op jit(solution)/shard_map/ppermute | solution.py:268
  49.6 14.8 %collective-permute-start.5 = (bf16[32,5120]{1,0:T(8,128)(2,1)S(1)}, bf16[32,5120]{1,0:T(8,128)(2,1)S(1)}, u32[]{:S(2)}, u32[]{:S(2)}) collective-permute-start(bf16[32,5120]{1,0:T(8,128)(2,1)S(1)} %get-tuple-element.10.refs_2_), channel_id=1, source_target_pairs={{0,1},{1,2},{2,3},{3,4},{4,5},{5,6},{6,7},{8,9},{9,10},{10,11},{11... | collective-permute-start | bytes 983048 | tf_op jit(solution)/shard_map/ppermute | solution.py:268
  52.4 17.0 %collective-permute-start.14 = (bf16[32,5120]{1,0:T(8,128)(2,1)S(1)}, bf16[32,5120]{1,0:T(8,128)(2,1)S(1)}, u32[]{:S(2)}, u32[]{:S(2)}) collective-permute-start(bf16[32,5120]{1,0:T(8,128)(2,1)S(1)} %get-tuple-element.9.refs_1_), channel_id=1, source_target_pairs={{1,0},{2,1},{3,2},{4,3},{5,4},{6,5},{7,6},{9,8},{10,9},{11,10},{12... | collective-permute-start | bytes 983048 | tf_op jit(solution)/shard_map/ppermute | solution.py:269
  55.4 16.7 %collective-permute-start.19 = (bf16[32,5120]{1,0:T(8,128)(2,1)S(1)}, bf16[32,5120]{1,0:T(8,128)(2,1)S(1)}, u32[]{:S(2)}, u32[]{:S(2)}) collective-permute-start(bf16[32,5120]{1,0:T(8,128)(2,1)S(1)} %get-tuple-element.10.refs_2_), channel_id=1, source_target_pairs={{1,0},{2,1},{3,2},{4,3},{5,4},{6,5},{7,6},{9,8},{10,9},{11,10},{12... | collective-permute-start | bytes 983048 | tf_op jit(solution)/shard_map/ppermute | solution.py:269
  58.0 16.8 %collective-permute-start.1 = (bf16[32,5120]{1,0:T(8,128)(2,1)S(1)}, bf16[32,5120]{1,0:T(8,128)(2,1)S(1)}, u32[]{:S(2)}, u32[]{:S(2)}) collective-permute-start(bf16[32,5120]{1,0:T(8,128)(2,1)S(1)} %collective-permute-done.refs_3_), channel_id=1, source_target_pairs={{1,2},{2,3},{3,4},{4,5},{5,6},{6,7},{9,10},{10,11},{11,12},{12,13}... | collective-permute-start | bytes 983048 | tf_op jit(solution)/shard_map/ppermute | solution.py:268
  64.3 11.9 %collective-permute-start.6 = (bf16[32,5120]{1,0:T(8,128)(2,1)S(1)}, bf16[32,5120]{1,0:T(8,128)(2,1)S(1)}, u32[]{:S(2)}, u32[]{:S(2)}) collective-permute-start(bf16[32,5120]{1,0:T(8,128)(2,1)S(1)} %collective-permute-done.5.refs_4_), channel_id=1, source_target_pairs={{1,2},{2,3},{3,4},{4,5},{5,6},{6,7},{9,10},{10,11},{11,12},{12,13}... | collective-permute-start | bytes 983048 | tf_op jit(solution)/shard_map/ppermute | solution.py:268
  69.5 10.0 %collective-permute-start.15 = (bf16[32,5120]{1,0:T(8,128)(2,1)S(1)}, bf16[32,5120]{1,0:T(8,128)(2,1)S(1)}, u32[]{:S(2)}, u32[]{:S(2)}) collective-permute-start(bf16[32,5120]{1,0:T(8,128)(2,1)S(1)} %collective-permute-done.14.refs_11_), channel_id=1, source_target_pairs={{1,0},{2,1},{3,2},{4,3},{5,4},{6,5},{9,8},{10,9},{11,10},{12,11},{... | collective-permute-start | bytes 983048 | tf_op jit(solution)/shard_map/ppermute | solution.py:269
  72.1 13.6 %collective-permute-start.20 = (bf16[32,5120]{1,0:T(8,128)(2,1)S(1)}, bf16[32,5120]{1,0:T(8,128)(2,1)S(1)}, u32[]{:S(2)}, u32[]{:S(2)}) collective-permute-start(bf16[32,5120]{1,0:T(8,128)(2,1)S(1)} %collective-permute-done.19.refs_12_), channel_id=1, source_target_pairs={{1,0},{2,1},{3,2},{4,3},{5,4},{6,5},{9,8},{10,9},{11,10},{12,11},{... | collective-permute-start | bytes 983048 | tf_op jit(solution)/shard_map/ppermute | solution.py:269
  74.8 16.1 %collective-permute-start.2 = (bf16[32,5120]{1,0:T(8,128)(2,1)S(1)}, bf16[32,5120]{1,0:T(8,128)(2,1)S(1)}, u32[]{:S(2)}, u32[]{:S(2)}) collective-permute-start(bf16[32,5120]{1,0:T(8,128)(2,1)S(1)} %collective-permute-done.1.refs_5_), channel_id=1, source_target_pairs={{2,3},{3,4},{4,5},{5,6},{6,7},{10,11},{11,12},{12,13},{13,14},{14,... | collective-permute-start | bytes 983048 | tf_op jit(solution)/shard_map/ppermute | solution.py:268
  76.2 16.1 %collective-permute-start.7 = (bf16[32,5120]{1,0:T(8,128)(2,1)S(1)}, bf16[32,5120]{1,0:T(8,128)(2,1)S(1)}, u32[]{:S(2)}, u32[]{:S(2)}) collective-permute-start(bf16[32,5120]{1,0:T(8,128)(2,1)S(1)} %collective-permute-done.6.refs_6_), channel_id=1, source_target_pairs={{2,3},{3,4},{4,5},{5,6},{6,7},{10,11},{11,12},{12,13},{13,14},{14,... | collective-permute-start | bytes 983048 | tf_op jit(solution)/shard_map/ppermute | solution.py:268
  79.4 17.4 %collective-permute-start.16 = (bf16[32,5120]{1,0:T(8,128)(2,1)S(1)}, bf16[32,5120]{1,0:T(8,128)(2,1)S(1)}, u32[]{:S(2)}, u32[]{:S(2)}) collective-permute-start(bf16[32,5120]{1,0:T(8,128)(2,1)S(1)} %collective-permute-done.15.refs_13_), channel_id=1, source_target_pairs={{1,0},{2,1},{3,2},{4,3},{5,4},{9,8},{10,9},{11,10},{12,11},{13,12}... | collective-permute-start | bytes 983048 | tf_op jit(solution)/shard_map/ppermute | solution.py:269
  85.7 18.2 %collective-permute-start.21 = (bf16[32,5120]{1,0:T(8,128)(2,1)S(1)}, bf16[32,5120]{1,0:T(8,128)(2,1)S(1)}, u32[]{:S(2)}, u32[]{:S(2)}) collective-permute-start(bf16[32,5120]{1,0:T(8,128)(2,1)S(1)} %collective-permute-done.20.refs_14_), channel_id=1, source_target_pairs={{1,0},{2,1},{3,2},{4,3},{5,4},{9,8},{10,9},{11,10},{12,11},{13,12}... | collective-permute-start | bytes 983048 | tf_op jit(solution)/shard_map/ppermute | solution.py:269
  90.8 15.7 %collective-permute-start.3 = (bf16[32,5120]{1,0:T(8,128)(2,1)S(1)}, bf16[32,5120]{1,0:T(8,128)(2,1)S(1)}, u32[]{:S(2)}, u32[]{:S(2)}) collective-permute-start(bf16[32,5120]{1,0:T(8,128)(2,1)S(1)} %collective-permute-done.2.refs_7_), channel_id=1, source_target_pairs={{3,4},{4,5},{5,6},{6,7},{11,12},{12,13},{13,14},{14,15},{19,20},{2... | collective-permute-start | bytes 983048 | tf_op jit(solution)/shard_map/ppermute | solution.py:268
  92.3 15.7 %collective-permute-start.8 = (bf16[32,5120]{1,0:T(8,128)(2,1)S(1)}, bf16[32,5120]{1,0:T(8,128)(2,1)S(1)}, u32[]{:S(2)}, u32[]{:S(2)}) collective-permute-start(bf16[32,5120]{1,0:T(8,128)(2,1)S(1)} %collective-permute-done.7.refs_8_), channel_id=1, source_target_pairs={{3,4},{4,5},{5,6},{6,7},{11,12},{12,13},{13,14},{14,15},{19,20},{2... | collective-permute-start | bytes 983048 | tf_op jit(solution)/shard_map/ppermute | solution.py:268
  96.9 14.0 %collective-permute-start.17 = (bf16[32,5120]{1,0:T(8,128)(2,1)S(1)}, bf16[32,5120]{1,0:T(8,128)(2,1)S(1)}, u32[]{:S(2)}, u32[]{:S(2)}) collective-permute-start(bf16[32,5120]{1,0:T(8,128)(2,1)S(1)} %collective-permute-done.16.refs_15_), channel_id=1, source_target_pairs={{1,0},{2,1},{3,2},{4,3},{9,8},{10,9},{11,10},{12,11},{17,16},{18,1... | collective-permute-start | bytes 983048 | tf_op jit(solution)/shard_map/ppermute | solution.py:269
  103.9 14.0 %collective-permute-start.22 = (bf16[32,5120]{1,0:T(8,128)(2,1)S(1)}, bf16[32,5120]{1,0:T(8,128)(2,1)S(1)}, u32[]{:S(2)}, u32[]{:S(2)}) collective-permute-start(bf16[32,5120]{1,0:T(8,128)(2,1)S(1)} %collective-permute-done.21.refs_16_), channel_id=1, source_target_pairs={{1,0},{2,1},{3,2},{4,3},{9,8},{10,9},{11,10},{12,11},{17,16},{18,1... | collective-permute-start | bytes 983048 | tf_op jit(solution)/shard_map/ppermute | solution.py:269
  106.6 14.0 %collective-permute-start.4 = (bf16[32,5120]{1,0:T(8,128)(2,1)S(1)}, bf16[32,5120]{1,0:T(8,128)(2,1)S(1)}, u32[]{:S(2)}, u32[]{:S(2)}) collective-permute-start(bf16[32,5120]{1,0:T(8,128)(2,1)S(1)} %collective-permute-done.3.refs_9_), channel_id=1, source_target_pairs={{4,5},{5,6},{6,7},{12,13},{13,14},{14,15},{20,21},{21,22},{22,23},... | collective-permute-start | bytes 983048 | tf_op jit(solution)/shard_map/ppermute | solution.py:268
  108.0 13.3 %collective-permute-start.9 = (bf16[32,5120]{1,0:T(8,128)(2,1)S(1)}, bf16[32,5120]{1,0:T(8,128)(2,1)S(1)}, u32[]{:S(2)}, u32[]{:S(2)}) collective-permute-start(bf16[32,5120]{1,0:T(8,128)(2,1)S(1)} %collective-permute-done.8.refs_10_), channel_id=1, source_target_pairs={{4,5},{5,6},{6,7},{12,13},{13,14},{14,15},{20,21},{21,22},{22,23},... | collective-permute-start | bytes 983048 | tf_op jit(solution)/shard_map/ppermute | solution.py:268
  110.9 14.0 %collective-permute-start.18 = (bf16[32,5120]{1,0:T(8,128)(2,1)S(1)}, bf16[32,5120]{1,0:T(8,128)(2,1)S(1)}, u32[]{:S(2)}, u32[]{:S(2)}) collective-permute-start(bf16[32,5120]{1,0:T(8,128)(2,1)S(1)} %collective-permute-done.17.refs_17_), channel_id=1, source_target_pairs={{1,0},{2,1},{3,2},{9,8},{10,9},{11,10},{17,16},{18,17},{19,18},{25... | collective-permute-start | bytes 983048 | tf_op jit(solution)/shard_map/ppermute | solution.py:269
  117.9 14.0 %collective-permute-start.23 = (bf16[32,5120]{1,0:T(8,128)(2,1)S(1)}, bf16[32,5120]{1,0:T(8,128)(2,1)S(1)}, u32[]{:S(2)}, u32[]{:S(2)}) collective-permute-start(bf16[32,5120]{1,0:T(8,128)(2,1)S(1)} %collective-permute-done.22.refs_18_), channel_id=1, source_target_pairs={{1,0},{2,1},{3,2},{9,8},{10,9},{11,10},{17,16},{18,17},{19,18},{25... | collective-permute-start | bytes 983048 | tf_op jit(solution)/shard_map/ppermute | solution.py:269
  120.6 13.3 %collective-permute-start.10 = (bf16[32,5120]{1,0:T(8,128)(2,1)S(1)}, bf16[32,5120]{1,0:T(8,128)(2,1)S(1)}, u32[]{:S(2)}, u32[]{:S(2)}) collective-permute-start(bf16[32,5120]{1,0:T(8,128)(2,1)S(1)} %collective-permute-done.4.refs_1_), channel_id=1, source_target_pairs={{5,6},{6,7},{13,14},{14,15},{21,22},{22,23},{29,30},{30,31},{37,38... | collective-permute-start | bytes 983048 | tf_op jit(solution)/shard_map/ppermute | solution.py:268
  121.3 14.0 %collective-permute-start.11 = (bf16[32,5120]{1,0:T(8,128)(2,1)S(1)}, bf16[32,5120]{1,0:T(8,128)(2,1)S(1)}, u32[]{:S(2)}, u32[]{:S(2)}) collective-permute-start(bf16[32,5120]{1,0:T(8,128)(2,1)S(1)} %collective-permute-done.9.refs_2_), channel_id=1, source_target_pairs={{5,6},{6,7},{13,14},{14,15},{21,22},{22,23},{29,30},{30,31},{37,38... | collective-permute-start | bytes 983048 | tf_op jit(solution)/shard_map/ppermute | solution.py:268
  124.9 11.8 %collective-permute-start.24 = (bf16[32,5120]{1,0:T(8,128)(2,1)S(1)}, bf16[32,5120]{1,0:T(8,128)(2,1)S(1)}, u32[]{:S(2)}, u32[]{:S(2)}) collective-permute-start(bf16[32,5120]{1,0:T(8,128)(2,1)S(1)} %collective-permute-done.18.refs_7_), channel_id=1, source_target_pairs={{1,0},{2,1},{9,8},{10,9},{17,16},{18,17},{25,24},{26,25},{33,32},{... | collective-permute-start | bytes 983048 | tf_op jit(solution)/shard_map/ppermute | solution.py:269
  132.0 10.0 %collective-permute-start.25 = (bf16[32,5120]{1,0:T(8,128)(2,1)S(1)}, bf16[32,5120]{1,0:T(8,128)(2,1)S(1)}, u32[]{:S(2)}, u32[]{:S(2)}) collective-permute-start(bf16[32,5120]{1,0:T(8,128)(2,1)S(1)} %collective-permute-done.23.refs_8_), channel_id=1, source_target_pairs={{1,0},{2,1},{9,8},{10,9},{17,16},{18,17},{25,24},{26,25},{33,32},{... | collective-permute-start | bytes 983048 | tf_op jit(solution)/shard_map/ppermute | solution.py:269
  133.9 56.4 %collective-permute-start.12 = (bf16[32,5120]{1,0:T(8,128)(2,1)S(1)}, bf16[32,5120]{1,0:T(8,128)(2,1)}, u32[]{:S(2)}, u32[]{:S(2)}) collective-permute-start(bf16[32,5120]{1,0:T(8,128)(2,1)S(1)} %collective-permute-done.10.refs_3_), channel_id=1, source_target_pairs={{6,7},{14,15},{22,23},{30,31},{38,39},{46,47},{54,55},{62,63},{70,... | collective-permute-start | bytes 983048 | tf_op jit(solution)/shard_map/ppermute | solution.py:268
  135.3 55.0 %collective-permute-start.13 = (bf16[32,5120]{1,0:T(8,128)(2,1)S(1)}, bf16[32,5120]{1,0:T(8,128)(2,1)}, u32[]{:S(2)}, u32[]{:S(2)}) collective-permute-start(bf16[32,5120]{1,0:T(8,128)(2,1)S(1)} %collective-permute-done.11.refs_4_), channel_id=1, source_target_pairs={{6,7},{14,15},{22,23},{30,31},{38,39},{46,47},{54,55},{62,63},{70,... | collective-permute-start | bytes 983048 | tf_op jit(solution)/shard_map/ppermute | solution.py:268
  136.7 53.6 %collective-permute-start.26 = (bf16[32,5120]{1,0:T(8,128)(2,1)S(1)}, bf16[32,5120]{1,0:T(8,128)(2,1)}, u32[]{:S(2)}, u32[]{:S(2)}) collective-permute-start(bf16[32,5120]{1,0:T(8,128)(2,1)S(1)} %collective-permute-done.24.refs_9_), channel_id=1, source_target_pairs={{1,0},{9,8},{17,16},{25,24},{33,32},{41,40},{49,48},{57,56},{65,64... | collective-permute-start | bytes 983048 | tf_op jit(solution)/shard_map/ppermute | solution.py:269
  142.0 48.3 %collective-permute-start.27 = (bf16[32,5120]{1,0:T(8,128)(2,1)S(1)}, bf16[32,5120]{1,0:T(8,128)(2,1)}, u32[]{:S(2)}, u32[]{:S(2)}) collective-permute-start(bf16[32,5120]{1,0:T(8,128)(2,1)S(1)} %collective-permute-done.25.refs_10_), channel_id=1, source_target_pairs={{1,0},{9,8},{17,16},{25,24},{33,32},{41,40},{49,48},{57,56},{65,64... | collective-permute-start | bytes 983048 | tf_op jit(solution)/shard_map/ppermute | solution.py:269
  147.1 3.7 %copy-start = (bf16[5376,896]{1,0:T(8,128)(2,1)S(1)}, bf16[5376,896]{1,0:T(8,128)(2,1)}, u32[]{:S(2)}) copy-start(bf16[5376,896]{1,0:T(8,128)(2,1)} %all-gather.3.cloned.1.call-done) | copy-start | bytes 28901380
  166.4 23.9 %copy-start.1 = (bf16[5376,896]{1,0:T(8,128)(2,1)S(1)}, bf16[5376,896]{1,0:T(8,128)(2,1)}, u32[]{:S(2)}) copy-start(bf16[5376,896]{1,0:T(8,128)(2,1)} %all-gather.3.cloned.1.call-done) | copy-start | bytes 28901380
  (34 other events, 30.2 us)
Sparse Core Ops, SparseCore 0:
  45.6 66.8 all-gather.2
